TPU v7x, 128 devices: a whole 4x4x4 slice. The times are simulated.
128 devices in a mesh: seg: 64 (over x, z_hi, y, core), dir: 2 (over z_lo).
Axes of the slice: x: 4, y: 4, z: 4 (z_hi: 2, z_lo: 2; z = z_hi * 2 + z_lo), core: 2. Of those that a mesh axis runs over, the one named last changes fastest.
Arguments:
- strain: float32 [512, 8, 6, 8192], P('seg'), may hold values from -16 to 16
- valid_flags: int32 [512, 8], P('seg'), may hold values from 0 to 1, as said below
- direction_ids: int32 [1024], P('dir'), may hold values from 0 to 3071
- grid_patterns: float32 [3072, 6], replicated, may hold values from -1 to 1
- grid_delays: float32 [3072, 3], replicated, may hold values from -40 to 40
Outputs:
- peak: float32 [8, 8192], P(None, 'seg')
- dir_score: float32 [8, 1024], P(None, 'dir')
Inputs may be any that keep to these rules, and one draw needn't show every extreme that they name: `valid_flags`: in every draw one window has no usable segment.
All inputs are finite; a program needn't handle non-finite values.
Results may differ from a plain program's by a relative error of at most 0.0001.
Values sent between devices are 32-bit elements; how exact they have to be, the bound alone decides.
A program may use at most 64 MiB of HBM per device.

v0:
```python
import math

import jax
import jax.numpy as jnp
from jax import lax
from jax.sharding import PartitionSpec as P

F = 8192


PAIRS = ((0, 1), (0, 2), (1, 2))


def in_blocks(array, dim, size):
    before, after = (array.shape[:dim], array.shape[dim + 1 :])
    return jnp.moveaxis(array.reshape(*before, size, -1, *after), dim, 0)


def sent_and_summed(array, axis, dim):
    tiles = in_blocks(array, dim, lax.axis_size(axis))
    arrived = lax.all_to_all(tiles, axis, split_axis=0, concat_axis=0, tiled=True)
    return arrived.sum(axis=0)


def from_everyone(array, axis):
    copies = jnp.broadcast_to(array, (lax.axis_size(axis), *array.shape))
    return lax.all_to_all(copies, axis, split_axis=0, concat_axis=0, tiled=True)


def laid_out(tiles, dim):
    dims = list(tiles.shape[1:])
    dims[dim] *= tiles.shape[0]
    return jnp.moveaxis(tiles, 0, dim).reshape(dims)


def gathered_copies(array, axis, dim):
    tiles = from_everyone(array, axis)
    return laid_out(tiles, dim)


def over_copies(array, axis):
    return from_everyone(array, axis).sum(axis=0)


def in_one(arrays, axis):
    flat, at, finished = (jnp.concatenate([a.reshape(-1) for a in arrays]), 0, [])
    so_far = over_copies(flat, axis)
    for a in arrays:
        finished.append(so_far[at : at + a.size].reshape(a.shape))
        at += a.size
    return tuple(finished)


def taken_together(array, axis):
    everything = from_everyone(array, axis)
    return jnp.max(everything, axis=0)


def spectra(strain, valid_flags):
    weight = valid_flags.astype(jnp.float32)[:, :, None]
    real_part = strain[:, :, 0:3, :]
    imag_part = strain[:, :, 3:6, :]
    parts = []
    for d in range(3):
        parts.append(
            jnp.sum(
                weight
                * (
                    real_part[:, :, d] * real_part[:, :, d]
                    + imag_part[:, :, d] * imag_part[:, :, d]
                ),
                0,
            )
        )
    for d, e in PAIRS:
        parts.append(
            jnp.sum(
                weight
                * (
                    real_part[:, :, d] * real_part[:, :, e]
                    + imag_part[:, :, d] * imag_part[:, :, e]
                ),
                0,
            )
        )
    for d, e in PAIRS:
        parts.append(
            jnp.sum(
                weight
                * (
                    imag_part[:, :, d] * real_part[:, :, e]
                    - real_part[:, :, d] * imag_part[:, :, e]
                ),
                0,
            )
        )
    return jnp.stack(parts, 0)


def null_vectors(rows):
    plus = rows[:, 0:3]
    cross = rows[:, 3:6]
    first = plus[:, 1] * cross[:, 2] - plus[:, 2] * cross[:, 1]
    second = plus[:, 2] * cross[:, 0] - plus[:, 0] * cross[:, 2]
    third = plus[:, 0] * cross[:, 1] - plus[:, 1] * cross[:, 0]
    null = jnp.stack([first, second, third], 1)
    norm2 = jnp.maximum(jnp.sum(null * null, 1), 0.25)
    return (null, norm2)


def project(cov, first_bin, null, norm2, delays, count, total_bins):
    width = cov.shape[2]
    freq = (first_bin + jnp.arange(width, dtype=jnp.int32)).astype(jnp.float32) * (
        2.0 * math.pi / total_bins
    )
    energy = jnp.zeros((null.shape[0], cov.shape[1], width), jnp.float32)
    for d in range(3):
        energy = energy + (null[:, d] * null[:, d])[:, None, None] * cov[d][None]
    for index, (d, e) in enumerate(PAIRS):
        angle = (delays[:, d] - delays[:, e])[:, None] * freq[None, :]
        factor = (2.0 * null[:, d] * null[:, e])[:, None, None]
        energy = energy + factor * (
            jnp.cos(angle)[:, None, :] * cov[3 + index][None]
            + jnp.sin(angle)[:, None, :] * cov[6 + index][None]
        )
    return energy / (norm2[:, None, None] * jnp.maximum(count, 1.0)[None, :, None])


def shards(strain, valid_flags, direction_ids, grid_patterns, grid_delays):
    windows = valid_flags.shape[1]
    grid_points = grid_patterns.shape[0]
    one_hot = (direction_ids[:, None] == jnp.arange(grid_points, dtype=jnp.int32)[None, :]).astype(
        jnp.float32
    )
    table = jnp.concatenate([grid_patterns, grid_delays], 1)
    picked = jnp.dot(
        one_hot, table, precision=lax.Precision.HIGHEST, preferred_element_type=jnp.float32
    )
    null, norm2 = null_vectors(picked[:, 0:6])
    delays = picked[:, 6:9]
    count_part = jnp.sum(valid_flags.astype(jnp.float32), 0)
    bin_share = F // lax.axis_size("seg")
    first_bin = lax.axis_index("seg") * bin_share
    own_windows = windows // lax.axis_size("dir")
    window_start = lax.axis_index("dir") * own_windows
    own_strain = lax.dynamic_slice_in_dim(strain, window_start, own_windows, 1)
    own_flags = lax.dynamic_slice_in_dim(valid_flags, window_start, own_windows, 1)
    own_cov = sent_and_summed(spectra(own_strain, own_flags), "seg", 2)
    cov = gathered_copies(own_cov, "dir", 1)
    unit = jnp.ones((windows,), jnp.float32)
    scaled = project(cov, first_bin, null, norm2, delays, unit, F)
    score_part = jnp.sum(scaled, 2) / F
    score_raw, count = in_one((score_part, count_part), "seg")
    divisor = jnp.maximum(count, 1.0)
    score = score_raw / divisor[None, :]
    peak_part = jnp.max(scaled, 0) / divisor[:, None]
    peak = taken_together(peak_part, "dir")
    return (peak, score.T)


def solution(mesh):
    placed = (P("seg", None, None, None), P("seg", None), P("dir"), P(), P())
    return jax.shard_map(
        shards,
        mesh=mesh,
        in_specs=placed,
        out_specs=(P(None, "seg"), P(None, "dir")),
        check_vma=False,
    )
```

profile of v0, /device:TPU:0, one launch (start us, length us, event | category | flops | bytes accessed | tf_op | source)
XLA Modules:
  0.0 95.0 jit_solution(18301728812046202096)
XLA Ops:
  0.6 0.8 dynamic-slice_convert_fusion
  1.4 8.0 %fusion.18 = (f32[4,8192]{1,0:T(4,128)S(1)}, f32[4,8192]{1,0:T(4,128)S(1)}, f32[4,8192]{1,0:T(4,128)S(1)}, f32[4,8192]{1,0:T(4,128)S(1)}, f32[4,8192]{1,0:T(4,12...) fusion(f32[8,8,6,8192]{3,1,2,0:T(8,128)} %param.5, ...), kind=kLoop, calls=%fused_computation.29 | loop fusion | flops 11501568 | bytes 7471256 | tf_op jit(solution)/shard_map/reduce_sum | solution.py:88
  9.4 0.7 bitcast_dynamic-update-slice_fusion.8
  10.0 0.7 bitcast_dynamic-update-slice_fusion.7
  10.7 0.7 bitcast_dynamic-update-slice_fusion.6
  11.4 0.7 bitcast_dynamic-update-slice_fusion.5
  12.1 0.7 bitcast_dynamic-update-slice_fusion.4
  12.8 0.7 bitcast_dynamic-update-slice_fusion.3
  13.5 0.7 bitcast_dynamic-update-slice_fusion.2
  14.2 0.7 bitcast_dynamic-update-slice_fusion.1
  14.9 0.7 bitcast_dynamic-update-slice_fusion
  15.6 11.4 %all-to-all-start = ((f32[64,9,4,128]{3,2,1,0:T(4,128)}), f32[64,9,4,128]{3,2,1,0:T(4,128)S(1)}, u32[]{:S(2)}, u32[]{:S(2)}) async-start(f32[64,9,4,128]{3,2,1,0:T(4,128)} %bitcast.26), calls=%async_computation | async-start | bytes 2359296 | tf_op jit(solution)/shard_map/all_to_all | solution.py:21
  27.0 3.0 %fusion = f32[512,9]{0,1:T(8,128)S(1)} fusion(s32[512]{0:T(512)S(1)} %copy-done.3, f32[3072,3]{0,1:T(4,128)S(1)} %copy-done.2, f32[3072,6]{0,1:T(8,128)S(1)} %copy-done.1), kind=kOutput, calls=%fused_computation.1 | convolution fusion | flops 171469824 | bytes 131072 | tf_op jit(solution)/shard_map/dot_general | solution.py:136
  30.1 2.8 %multiply_cosine_fusion.2 = (f32[512,128]{1,0:T(8,128)S(1)}, f32[512,128]{1,0:T(8,128)S(1)}, f32[512,128]{1,0:T(8,128)S(1)}, f32[512,128]{1,0:T(8,128)S(1)}, f32[512,128]{1,0:T(8,128)S(1)}, /*index=5*/f32[512,128]{1,0:T(8,128)S(1)}) fusion(f32[128]{0:T(128)S(1)} %convert_multiply_fusion, f32[512]{0:T(512)S(1)} %bitcast.208, f32[512]{0:T(512)S(1)} %bitcast.209, ...), kind=kLoop, calls=%fused_computation.51 | loop fusion | flops 196608 | bytes 1579520 | tf_op jit(solution)/shard_map/cos | solution.py:123
  32.9 14.6 %all-to-all-done = f32[64,9,4,128]{3,2,1,0:T(4,128)S(1)} async-done(((f32[64,9,4,128]{3,2,1,0:T(4,128)}), f32[64,9,4,128]{3,2,1,0:T(4,128)S(1)}, u32[]{:S(2)}, u32[]{:S(2)}) %all-to-all-start) | async-done | bytes 1179680 | tf_op jit(solution)/shard_map/all_to_all | solution.py:21
  47.7 0.6 broadcast_in_dim.6
  48.3 3.3 %all-to-all-start.1 = ((f32[2,9,4,128]{3,2,1,0:T(4,128)}), f32[2,9,4,128]{3,2,1,0:T(4,128)S(1)}, u32[]{:S(2)}, u32[]{:S(2)}) async-start(f32[2,9,4,128]{3,2,1,0:T(4,128)} %broadcast_in_dim.6), calls=%async_computation.1 | async-start | bytes 73728 | tf_op jit(solution)/shard_map/all_to_all | solution.py:27
  51.6 3.9 %all-to-all-done.1 = f32[2,9,4,128]{3,2,1,0:T(4,128)S(1)} async-done(((f32[2,9,4,128]{3,2,1,0:T(4,128)}), f32[2,9,4,128]{3,2,1,0:T(4,128)S(1)}, u32[]{:S(2)}, u32[]{:S(2)}) %all-to-all-start.1) | async-done | bytes 36896 | tf_op jit(solution)/shard_map/all_to_all | solution.py:27
  55.5 5.3 %fusion.31 = (f32[512,8]{1,0:T(8,128)S(1)}, f32[8,128]{1,0:T(8,128)S(1)}) fusion(f32[512]{0:T(512)S(1)} %broadcast_maximum_fusion, f32[8,128]{1,0:T(8,128)S(1)} %bitcast.200, f32[512,128]{1,0:T(8,128)S(1)} %get-tuple-element.52, f32[8,128]{1,0:T(8,128)S(1)} %bitcast.201, f32[512,128]{1,0:T(8,128)S(1)} %get-tuple-element.53, f32[512]{0:T(512)S(1)} %get-tuple-element.54, ...), kind=kLoop, calls=%fused_computation.84 | loop fusion | flops 12053504 | bytes 1644544 | tf_op jit(solution)/shard_map/reduce_sum | solution.py:152
  61.6 24.3 %all_to_all.21 = f32[64,1,4104]{2,1,0:T(1,128)S(1)} all-to-all(f32[64,1,4104]{2,1,0:T(1,128)S(1)} %broadcast_in_dim.7), channel_id=1, replica_groups=mesh['seg'=64,'dir'=2] {'seg'}, dimensions={0} | all-to-all | bytes 2101248 | tf_op jit(solution)/shard_map/all_to_all | solution.py:27
  85.8 0.7 reduce_sum.139
  87.4 3.2 %all-to-all-start.3 = ((f32[2,8,128]{2,1,0:T(8,128)}), f32[2,8,128]{2,1,0:T(8,128)S(1)}, u32[]{:S(2)}, u32[]{:S(2)}) async-start(f32[2,8,128]{2,1,0:T(8,128)} %broadcast_in_dim.8), calls=%async_computation.3 | async-start | bytes 16384 | tf_op jit(solution)/shard_map/all_to_all | solution.py:27
  90.6 0.7 copy.71
  91.3 3.1 %all-to-all-done.3 = f32[2,8,128]{2,1,0:T(8,128)S(1)} async-done(((f32[2,8,128]{2,1,0:T(8,128)}), f32[2,8,128]{2,1,0:T(8,128)S(1)}, u32[]{:S(2)}, u32[]{:S(2)}) %all-to-all-start.3) | async-done | bytes 8224 | tf_op jit(solution)/shard_map/all_to_all | solution.py:27
  (28 shorter events, 2.5 us)
Async XLA Ops:
  10.7 16.2 %copy-start.1 = (f32[3072,6]{0,1:T(8,128)S(1)}, f32[3072,6]{0,1:T(8,128)}, u32[]{:S(2)}) copy-start(f32[3072,6]{0,1:T(8,128)} %param.8) | copy-start | bytes 221188
  10.7 16.2 %copy-start.2 = (f32[3072,3]{0,1:T(4,128)S(1)}, f32[3072,3]{0,1:T(4,128)}, u32[]{:S(2)}) copy-start(f32[3072,3]{0,1:T(4,128)} %param.9) | copy-start | bytes 110596
  10.7 16.2 %copy-start.3 = (s32[512]{0:T(512)S(1)}, s32[512]{0:T(512)}, u32[]{:S(2)}) copy-start(s32[512]{0:T(512)} %param.7) | copy-start | bytes 6148
  15.6 31.9 %all-to-all-start = ((f32[64,9,4,128]{3,2,1,0:T(4,128)}), f32[64,9,4,128]{3,2,1,0:T(4,128)S(1)}, u32[]{:S(2)}, u32[]{:S(2)}) async-start(f32[64,9,4,128]{3,2,1,0:T(4,128)} %bitcast.26), calls=%async_computation | async-start | bytes 2359296 | tf_op jit(solution)/shard_map/all_to_all | solution.py:21
  27.0 24.6 %copy-start = (s32[8,8]{1,0:T(8,128)S(1)}, s32[8,8]{1,0:T(8,128)}, u32[]{:S(2)}) copy-start(s32[8,8]{1,0:T(8,128)} %param.6) | copy-start | bytes 772
  48.3 7.2 %all-to-all-start.1 = ((f32[2,9,4,128]{3,2,1,0:T(4,128)}), f32[2,9,4,128]{3,2,1,0:T(4,128)S(1)}, u32[]{:S(2)}, u32[]{:S(2)}) async-start(f32[2,9,4,128]{3,2,1,0:T(4,128)} %broadcast_in_dim.6), calls=%async_computation.1 | async-start | bytes 73728 | tf_op jit(solution)/shard_map/all_to_all | solution.py:27
  87.4 7.0 %all-to-all-start.3 = ((f32[2,8,128]{2,1,0:T(8,128)}), f32[2,8,128]{2,1,0:T(8,128)S(1)}, u32[]{:S(2)}, u32[]{:S(2)}) async-start(f32[2,8,128]{2,1,0:T(8,128)} %broadcast_in_dim.8), calls=%async_computation.3 | async-start | bytes 16384 | tf_op jit(solution)/shard_map/all_to_all | solution.py:27
where the time goes:
time: 95.4 us; the launch traced here: 95 us
  blocking collectives  24.3 us (25%)
  waiting for transfers between devices  21.6 us (23%)
  other arithmetic  18.5 us (19%)
  starting transfers between devices  17.8 us (19%)
  local copies, waits for them, and re-layouts  9.01 us (9%)
  matrix products  2.97 us (3%)
    all_to_all x1, blocking collectives, from_everyone(): return lax.all_to_all(copies, axis, split_axis=0, concat_axis=0, tiled=True)  24.3 us
    all_to_all x1, waiting for transfers between devices, sent_and_summed(): lax.all_to_all(tiles, axis, split_axis=0, concat_axis=0, tiled=True)  14.6 us
    all_to_all x1, starting transfers between devices, sent_and_summed(): lax.all_to_all(tiles, axis, split_axis=0, concat_axis=0, tiled=True)  11.4 us
    reduce_sum x1, other arithmetic, spectra(): jnp.sum(weight * (imag_part[:, :, d] * real_part[:, :, e] - real_part[:,...  7.97 us
    all_to_all x2, waiting for transfers between devices, from_everyone(): return lax.all_to_all(copies, axis, split_axis=0, concat_axis=0, tiled=True)  6.98 us
    all_to_all x2, starting transfers between devices, from_everyone(): return lax.all_to_all(copies, axis, split_axis=0, concat_axis=0, tiled=True)  6.48 us
    unnamed x17, local copies, waits for them, and re-layouts  6.25 us
    reduce_sum x1, other arithmetic, shards(): score_part = jnp.sum(scaled, 2) / F  5.27 us
  transfers between devices with their start and end apart: 3, of which 3 were waited for; matrix products, arithmetic and copies ran while one was open for 7% of the time, Pallas kernels for 0%

commit v1 on v0

v1 whole, which is shorter than its diff:
```python
import functools
import math

import jax
import jax.numpy as jnp
from jax import lax
from jax.experimental import pallas as pl
from jax.experimental.pallas import tpu as pltpu
from jax.sharding import PartitionSpec as P

F = 8192
PAIRS = ((0, 1), (0, 2), (1, 2))
FAR_FIRST = (2, 1, 3, 0)
MESH = pl.DeviceIdType.MESH
F32 = jnp.float32

SIN = [(-1.0) ** n * math.pi ** (2 * n + 1) / math.factorial(2 * n + 1) for n in range(7)]
COS = [(-1.0) ** n * math.pi ** (2 * n) / math.factorial(2 * n) for n in range(8)]


def horner(coefs, y):
    total = jnp.full_like(y, coefs[-1])
    for c in reversed(coefs[:-1]):
        total = total * y + c
    return total


def sincos_turns(u):
    r = u - jnp.round(u)
    y = r * r
    s = r * horner(SIN, y)
    c = horner(COS, y)
    return 2.0 * s * c, 1.0 - 2.0 * s * s


def kernel(
    strain, flags, ids, patterns, delays, peak_out, score_out,
    sb, part, cbuf, red, p1buf, s2buf, p2buf, plane, zbuf, cov,
    fl, idv, pat, dly, mask, lhs, coef, tab,
    acc, rbuf, pk, pkr,
    in_sem, st_sem, cs, cr, p1s, p1r, p2s, p2r, zs, zr, ds_, dr, es, er,
):
    me = lax.axis_index("seg")
    d = lax.axis_index("dir")
    core = lax.rem(me, 2)
    y = lax.rem(me // 2, 4)
    h = lax.rem(me // 8, 2)
    x = me // 16
    a = x + core * (y - x)
    b = y + core * (x - y)
    stride_a = 16 - 14 * core
    stride_b = 2 + 14 * core
    me_core = me + 1 - 2 * core
    me_h = me + 8 - 16 * h
    me_core_h = me_core + 8 - 16 * h

    def remote(src, dst, ssem, rsem, seg, dr_):
        return pltpu.make_async_remote_copy(
            src_ref=src, dst_ref=dst, send_sem=ssem, recv_sem=rsem,
            device_id=(seg, dr_), device_id_type=MESH)

    def along(j, at, stride):
        return me + (lax.rem(at + j, 4) - at) * stride

    barrier = pltpu.get_barrier_semaphore()
    friends = [(me_core, d), (me_h, d), (me, 1 - d), (me_h, 1 - d), (me_core_h, d)]
    for j in (1, 2, 3):
        friends += [(along(j, x, 16), d), (along(j, y, 2), d)]

    smalls = [
        pltpu.make_async_copy(flags, fl, in_sem.at[0]),
        pltpu.make_async_copy(ids, idv, in_sem.at[1]),
        pltpu.make_async_copy(patterns, pat, in_sem.at[2]),
        pltpu.make_async_copy(delays, dly, in_sem.at[3]),
    ]
    smalls[0].start()

    def chunk_copy(i, s):
        xp = lax.rem(x + FAR_FIRST[i], 4)
        start = pl.multiple_of((xp * 2 + d) * 1024, 1024)
        return pltpu.make_async_copy(
            strain.at[s, :, :, pl.ds(start, 1024)], sb.at[i, s], st_sem.at[i, s])

    for i in range(4):
        for s in range(8):
            chunk_copy(i, s).start()
    for c in smalls[1:]:
        c.start()
    for seg, dr_ in friends:
        pl.semaphore_signal(barrier, inc=1, device_id=(seg, dr_), device_id_type=MESH)

    smalls[0].wait()
    lane = lax.broadcasted_iota(jnp.int32, (8, 128), 1)
    sub8 = lax.broadcasted_iota(jnp.int32, (8, 8), 0)
    lane8 = lax.broadcasted_iota(jnp.int32, (8, 8), 1)
    fv = fl[...].astype(F32)
    count = jnp.zeros((8, 128), F32)
    for s in range(8):
        row = jnp.broadcast_to(fv[s : s + 1, :], (8, 8))
        col = jnp.sum(jnp.where(sub8 == lane8, row, 0.0), axis=1, keepdims=True)
        m = jnp.broadcast_to(col, (8, 128))
        mask[s] = m
        count = count + m

    def spectra(i, cc):
        def one(yp, carry):
            q = pl.multiple_of((yp * 2 + cc) * 128, 128)
            tot = [None] * 9

            def add(k, v):
                tot[k] = v if tot[k] is None else tot[k] + v

            for s in range(8):
                m = mask[s]
                re = [sb[i, s, e, :, pl.ds(q, 128)] * m for e in range(3)]
                im = [sb[i, s, e + 3, :, pl.ds(q, 128)] * m for e in range(3)]
                for e in range(3):
                    add(e, re[e] * re[e] + im[e] * im[e])
                for n, (e, g) in enumerate(PAIRS):
                    add(3 + n, re[e] * re[g] + im[e] * im[g])
                    add(6 + n, im[e] * re[g] - re[e] * im[g])
            for k in range(9):
                part[i, cc, yp, k] = tot[k]
            return carry

        lax.fori_loop(0, 4, one, 0)

    def core_copy(i):
        return remote(part.at[i, 1 - core], cbuf.at[i], cs.at[i], cr.at[i], me_core, d)

    def unit(i, j):
        xp = lax.rem(x + FAR_FIRST[i], 4)
        return xp + core * (j - xp), j + core * (xp - j)

    def p1_copy(i, j):
        ap, bp = unit(i, j)
        slot = lax.rem(ap - a + 4, 4) - 1
        return remote(red.at[ap, bp], p1buf.at[slot, bp], p1s.at[slot, bp],
                      p1r.at[slot, bp], me + (ap - a) * stride_a, d)

    def core_reduce(i):
        core_copy(i).wait_recv()
        for j in range(4):
            ap, bp = unit(i, j)
            red[ap, bp] = part[i, core, j] + cbuf[i, j]
        for j in range(4):
            ap, bp = unit(i, j)

            @pl.when(ap != a)
            def _():
                p1_copy(i, j).start()

    for i in range(4):
        for s in range(8):
            chunk_copy(i, s).wait()
        spectra(i, 1 - core)
        if i == 0:
            pl.semaphore_wait(barrier, len(friends))
        core_copy(i).start()
        spectra(i, core)
        if i > 0:
            core_reduce(i - 1)
    core_reduce(3)

    for c in smalls[1:]:
        c.wait()
    lhs[...] = jnp.zeros_like(lhs)
    for n, (src, rows) in enumerate(((pat, 6), (dly, 3))):
        v = src[...]
        hi = v.astype(jnp.bfloat16).astype(F32)
        rest = v - hi
        mid = rest.astype(jnp.bfloat16).astype(F32)
        lo = rest - mid
        lhs[8 * n : 8 * n + rows] = hi
        lhs[16 + 8 * n : 16 + 8 * n + rows] = mid
        lhs[32 + 8 * n : 32 + 8 * n + rows] = lo
    idrow = idv[...]

    def pick(g, got):
        base = pl.multiple_of(g * 256, 256)
        at = lax.broadcasted_iota(jnp.int32, (256, 512), 0) + base
        hot = jnp.where(at == idrow, 1.0, 0.0).astype(jnp.bfloat16)
        left = lhs[:, pl.ds(base, 256)].astype(jnp.bfloat16)
        return got + jnp.dot(left, hot, preferred_element_type=F32)

    got = lax.fori_loop(0, 12, pick, jnp.zeros((48, 512), F32))
    got = got[0:16] + got[16:32] + got[32:48]
    p = [got[n : n + 1] for n in range(6)]
    t = [got[8 + n : 9 + n] for n in range(3)]
    null = [
        p[1] * p[5] - p[2] * p[4],
        p[2] * p[3] - p[0] * p[5],
        p[0] * p[4] - p[1] * p[3],
    ]
    norm2 = jnp.maximum(null[0] * null[0] + null[1] * null[1] + null[2] * null[2], 0.25)
    inv = 1.0 / norm2
    rows = [n * n * inv for n in null]
    rows += [2.0 * null[e] * null[g] * inv for e, g in PAIRS]
    block = me.astype(F32) * (1.0 / 64.0)
    lags = [t[e] - t[g] for e, g in PAIRS]
    firsts = [v * block for v in lags]
    rows += [v - jnp.round(v) for v in firsts]
    rows += [v * (1.0 / F) for v in lags]
    rows += [jnp.zeros_like(inv)] * 4
    coef[...] = jnp.concatenate(rows, axis=0).T
    lanef = lane.astype(F32)

    def tables(g, carry):
        k = pl.multiple_of(g * 8, 8)
        c = coef[pl.ds(k, 8), :]

        def wide(n):
            return jnp.broadcast_to(c[:, n : n + 1], (8, 128))

        for n in range(3):
            tab[n, pl.ds(k, 8), :] = wide(n)
            sn, cn = sincos_turns(wide(6 + n) + wide(9 + n) * lanef)
            w = wide(3 + n)
            tab[3 + n, pl.ds(k, 8), :] = w * cn
            tab[6 + n, pl.ds(k, 8), :] = w * sn
        return carry

    lax.fori_loop(0, 64, tables, 0)

    def p1_wait(slot, bp):
        remote(red.at[a, bp], p1buf.at[slot, bp], p1s.at[slot, bp],
               p1r.at[slot, bp], me, d).wait_recv()

    def p2_copy(o):
        return remote(s2buf.at[o - 1], p2buf.at[o - 1], p2s.at[o - 1], p2r.at[o - 1],
                      along(o, b, stride_b), d)

    for o in (2, 1, 3):
        bp = lax.rem(b + o, 4)
        for slot in range(3):
            p1_wait(slot, bp)
        s2buf[o - 1] = (red[a, bp] + p1buf[0, bp]) + (p1buf[1, bp] + p1buf[2, bp])
        p2_copy(o).start()
    for slot in range(3):
        p1_wait(slot, b)
    own = (red[a, b] + p1buf[0, b]) + (p1buf[1, b] + p1buf[2, b])
    for o in (1, 2, 3):
        p2_copy(o).wait_recv()
    plane[...] = (own + p2buf[0]) + (p2buf[1] + p2buf[2])

    def z_copy(dd, n):
        return remote(plane, zbuf.at[h], zs.at[n], zr.at[h], me + (d - h) * 8, dd)

    @pl.when(h == d)
    def _():
        z_copy(1 - d, 0).start()

    @pl.when(h != d)
    def _():
        z_copy(0, 0).start()
        z_copy(1, 1).start()

    def z_wait(slot):
        remote(plane, zbuf.at[slot], zs.at[0], zr.at[slot], me, d).wait_recv()

    @pl.when(h == d)
    def _():
        z_wait(1 - h)
        cov[...] = plane[...] + zbuf[1 - h]

    @pl.when(h != d)
    def _():
        z_wait(0)
        z_wait(1)
        cov[...] = zbuf[0] + zbuf[1]

    cv = [cov[n] for n in range(9)]

    def outer(o, best):
        def inner(g, carry):
            best, score = carry
            for kk in range(8):
                k = o * 128 + g * 8 + kk
                e = None
                for n in range(9):
                    w = jnp.broadcast_to(tab[n, pl.ds(k, 1), :], (8, 128))
                    v = w * cv[n]
                    e = v if e is None else e + v
                best = jnp.maximum(best, e)
                s = jnp.sum(e, axis=1, keepdims=True)
                score = jnp.where(lane == g * 8 + kk, s, score)
            return best, score

        best, score = lax.fori_loop(0, 16, inner, (best, jnp.zeros((8, 128), F32)))
        acc[0, :, pl.ds(pl.multiple_of(o * 128, 128), 128)] = score
        return best

    best = lax.fori_loop(0, 4, outer, jnp.full((8, 128), -jnp.inf, F32))
    acc[0, :, 512:640] = count
    pk[...] = best

    pk_copy = remote(pk, pkr, es, er, me, 1 - d)
    pk_copy.start()

    groups = (
        ((me_core, 0), (me_h, 1), (me_core_h, 2)),
        tuple((along(o, a, stride_a), o - 1) for o in (2, 1, 3)),
        tuple((along(o, b, stride_b), o - 1) for o in (2, 1, 3)),
    )
    for n, group in enumerate(groups):
        copies = [
            remote(acc.at[n], rbuf.at[n, slot], ds_.at[n, slot], dr.at[n, slot], seg, d)
            for seg, slot in group
        ]
        for c in copies:
            c.start()
        for c in copies:
            c.wait_recv()
        acc[n + 1] = (acc[n] + rbuf[n, 0]) + (rbuf[n, 1] + rbuf[n, 2])

    inv_count = 1.0 / jnp.maximum(acc[3, :, 512:640], 1.0)
    for o in range(4):
        score_out[:, 128 * o : 128 * o + 128] = acc[3, :, 128 * o : 128 * o + 128] * inv_count * (1.0 / F)
    pk_copy.wait_recv()
    peak_out[...] = jnp.maximum(best, pkr[...]) * inv_count

    for i in range(4):
        core_copy(i).wait_send()
    for slot in range(3):
        for bp in range(4):
            remote(red.at[a, bp], p1buf.at[slot, bp], p1s.at[slot, bp],
                   p1r.at[slot, bp], me, d).wait_send()
    for o in (1, 2, 3):
        p2_copy(o).wait_send()
    z_copy(0, 0).wait_send()

    @pl.when(h != d)
    def _():
        z_copy(1, 1).wait_send()

    pk_copy.wait_send()
    for n, group in enumerate(groups):
        for seg, slot in group:
            remote(acc.at[n], rbuf.at[n, slot], ds_.at[n, slot], dr.at[n, slot], seg, d).wait_send()


def shards(strain, valid_flags, direction_ids, grid_patterns, grid_delays):
    unit = (9, 8, 128)
    dma = pltpu.SemaphoreType.DMA
    anywhere = pl.BlockSpec(memory_space=pl.ANY)
    vmem = pl.BlockSpec(memory_space=pltpu.VMEM)
    return pl.pallas_call(
        kernel,
        out_shape=(
            jax.ShapeDtypeStruct((8, 128), F32),
            jax.ShapeDtypeStruct((8, 512), F32),
        ),
        in_specs=[anywhere] * 5,
        out_specs=(vmem, vmem),
        scratch_shapes=[
            pltpu.VMEM((4, 8, 6, 8, 1024), F32),
            pltpu.VMEM((4, 2, 4) + unit, F32),
            pltpu.VMEM((4, 4) + unit, F32),
            pltpu.VMEM((4, 4) + unit, F32),
            pltpu.VMEM((3, 4) + unit, F32),
            pltpu.VMEM((3,) + unit, F32),
            pltpu.VMEM((3,) + unit, F32),
            pltpu.VMEM(unit, F32),
            pltpu.VMEM((2,) + unit, F32),
            pltpu.VMEM(unit, F32),
            pltpu.VMEM((8, 8), jnp.int32),
            pltpu.VMEM((1, 512), jnp.int32),
            pltpu.VMEM((6, 3072), F32),
            pltpu.VMEM((3, 3072), F32),
            pltpu.VMEM((8, 8, 128), F32),
            pltpu.VMEM((48, 3072), F32),
            pltpu.VMEM((512, 16), F32),
            pltpu.VMEM((9, 512, 128), F32),
            pltpu.VMEM((4, 8, 640), F32),
            pltpu.VMEM((3, 3, 8, 640), F32),
            pltpu.VMEM((8, 128), F32),
            pltpu.VMEM((8, 128), F32),
            dma((4,)), dma((4, 8)),
            dma((4,)), dma((4,)),
            dma((3, 4)), dma((3, 4)),
            dma((3,)), dma((3,)),
            dma((2,)), dma((2,)),
            dma((3, 3)), dma((3, 3)),
            dma(()), dma(()),
        ],
        compiler_params=pltpu.CompilerParams(collective_id=0, has_side_effects=True),
        name="sky",
    )(
        strain.transpose(0, 2, 1, 3),
        valid_flags,
        direction_ids.reshape(1, -1),
        grid_patterns.T,
        grid_delays.T,
    )


def solution(mesh):
    placed = (P("seg", None, None, None), P("seg", None), P("dir"), P(), P())
    return jax.shard_map(
        shards,
        mesh=mesh,
        in_specs=placed,
        out_specs=(P(None, "seg"), P(None, "dir")),
        check_vma=False,
    )
```

time: 95.4 us -> 48.7 us (0.51)
  Pallas kernels: 0 us -> 45.2 us
  blocking collectives: 24.3 us -> 0 us
  waiting for transfers between devices: 21.6 us -> 0 us
  other arithmetic: 18.5 us -> 0 us
  starting transfers between devices: 17.8 us -> 0 us
  local copies, waits for them, and re-layouts: 9.01 us -> 2.59 us
  matrix products: 2.97 us -> 0 us
    pallas_call x0 -> x1, Pallas kernels: none -> 45.2 us  [shards(): pl.pallas_call(kernel, out_shape=(jax.ShapeDtypeStruct((8, 128), F32), ja...]
    all_to_all x1 -> x0, blocking collectives: 24.3 us -> none  [from_everyone(): return lax.all_to_all(copies, axis, split_axis=0, concat_axis=0, tiled=True)]
    all_to_all x3 -> x0, waiting for transfers between devices: 21.6 us -> none  [the longest x1 14.6 us: sent_and_summed(): lax.all_to_all(tiles, axis, split_axis=0, concat_axis=0, tiled=True)]
    all_to_all x3 -> x0, starting transfers between devices: 17.8 us -> none  [the longest x1 11.4 us: sent_and_summed(): lax.all_to_all(tiles, axis, split_axis=0, concat_axis=0, tiled=True)]
    reduce_sum x6 -> x0, other arithmetic: 14.1 us -> none  [the longest x1 7.97 us: spectra(): jnp.sum(weight * (imag_part[:, :, d] * real_part[:, :, e] - real_part[:,...]
    unnamed x17 -> x2, local copies, waits for them, and re-layouts: 6.25 us -> 2.59 us
    dot_general x1 -> x0, matrix products: 2.97 us -> none  [shards(): jnp.dot(one_hot, table, precision=lax.Precision.HIGHEST, preferred_elemen...]
    cos x1 -> x0, other arithmetic: 2.79 us -> none  [project(): jnp.cos(angle)[:, None, :] * cov[3 + index][None]]
  transfers between devices with their start and end apart: 3 -> 0, of which waited for: 3 -> 0; matrix products, arithmetic and copies ran while one was open for 7% -> 0% of each run, Pallas kernels for 0% -> 0%
where the time goes in v1:
time: 48.7 us; the launch traced here: 48.5 us
  Pallas kernels  45.2 us (93%)
  local copies, waits for them, and re-layouts  2.59 us (5%)
  between operations  0.64 us (1%)
    pallas_call x1, Pallas kernels, shards(): pl.pallas_call(kernel, out_shape=(jax.ShapeDtypeStruct((8, 128), F32), ja...  45.2 us
    unnamed x2, local copies, waits for them, and re-layouts  2.59 us

profile of v1, /device:TPU:0, one launch (start us, length us, event | category | flops | bytes accessed | tf_op | source)
XLA Modules:
  0.0 48.5 jit_solution(12977444851682200359)
XLA Ops:
  0.6 45.2 %sky.1 = (f32[8,128]{1,0:T(8,128)}, f32[8,512]{1,0:T(8,128)}) custom-call(f32[8,6,8,8192]{3,2,1,0:T(8,128)} %bitcast.4, s32[8,8]{1,0:T(8,128)} %flags.1, s32[1,512]{1,0:T(1,128)} %bitcast.7, f32[6,3072]{1,0:T(8,128)} %bitcast.5, f32[3,3072]{1,0:T(4,128)} %bitcast.6), custom_call_target="tpu_custom_call" | custom-call | tf_op jit(solution)/shard_map/sky/pallas_call | solution.py:347
  45.9 1.3 %copy.9 = f32[8,128]{1,0:T(8,128)} copy(f32[8,128]{1,0:T(8,128)} %get-tuple-element.4) | data formatting | bytes 8192
  47.1 1.3 %copy.10 = f32[8,512]{1,0:T(8,128)} copy(f32[8,512]{1,0:T(8,128)} %get-tuple-element.5) | data formatting | bytes 32768
